TPU v7x, 32 devices: a whole 2x2x4 slice. The times are simulated.
32 devices in a mesh: segment: 4 (over y, core), dp: 8 (over z, x).
Axes of the slice: x: 2, y: 2, z: 4, core: 2. Of those that a mesh axis runs over, the one named last changes fastest.
Arguments:
- token_ids: int32 [1024], P('dp'), may hold values from 0 to 38015, as said below
- table: bfloat16 [4752, 28672], P('segment', 'dp'), may hold values from -6 to 6
- out_grad: bfloat16 [1024, 3584], P('dp', 'segment'), may hold values from -6 to 6
Outputs:
- embedded: bfloat16 [1024, 3584], P('dp')
- table_grad: bfloat16 [4752, 28672], P('segment', 'dp')
Inputs may be any that keep to these rules, and one draw needn't show every extreme that they name: `token_ids`: in the 128 tokens of each data group, at most 16 ids lie in one segment's slice of 9504 rows with one residue modulo 8; in every data group some segment and residue has exactly 16.
All inputs are finite; a program needn't handle non-finite values.
Results may differ from a plain program's by a relative error of at most 0.001.
Values may be sent and summed in bfloat16 or wider, within the bound.
A program may use at most 64 MiB of HBM per device.

v0:
```python
import jax
import jax.numpy as jnp
from jax import lax
from jax.sharding import PartitionSpec as P

D = 3584
PACK = 8


def body(token_ids, table, out_grad):
    lines = table.shape[0]
    width = table.shape[1]
    groups = lax.axis_size("dp")
    tok_rows = token_ids.shape[0]
    quarters = D // width
    slot = lax.axis_index("dp") // quarters
    first = lax.axis_index("segment") * lines * PACK
    every_id = lax.all_gather(token_ids, "dp", axis=0, tiled=True)
    local = every_id - first
    in_section = (local >= 0) & (local < lines * PACK)
    owned = in_section & (local % PACK == slot)
    line_idx = jnp.clip(local // PACK, 0, lines - 1)
    whole_grad = lax.all_gather(out_grad, "segment", axis=1, tiled=True)
    capacity = tok_rows // PACK
    owned_grid = owned.reshape(groups, tok_rows)
    rank = jnp.cumsum(owned_grid.astype(jnp.int32), axis=1) - 1
    place = jnp.where(owned_grid, rank, capacity)
    group_rows = jnp.broadcast_to(jnp.arange(groups, dtype=jnp.int32)[:, None], (groups, tok_rows))
    row_of = (
        jnp.zeros((groups, capacity), jnp.int32)
        .at[group_rows, place]
        .set(line_idx.reshape(groups, tok_rows), mode="drop")
    )
    filled = jnp.zeros((groups, capacity), jnp.bool_).at[group_rows, place].set(True, mode="drop")
    fetched = jnp.take(table, row_of.reshape(-1), axis=0).reshape(groups, capacity, width)
    fetched = jnp.where(filled[:, :, None], fetched, jnp.zeros((), jnp.bfloat16))
    arrived = lax.all_to_all(fetched, "dp", split_axis=0, concat_axis=0, tiled=True)
    my_local = token_ids - first
    my_in = (my_local >= 0) & (my_local < lines * PACK)
    my_slot = my_local % PACK
    slot_hits = (my_slot[:, None] == jnp.arange(PACK, dtype=jnp.int32)[None, :]) & my_in[:, None]
    slot_ranks = jnp.cumsum(slot_hits.astype(jnp.int32), axis=0) - 1
    my_rank = jnp.sum(jnp.where(slot_hits, slot_ranks, 0), axis=1)
    sources = my_slot[:, None] * quarters + jnp.arange(quarters, dtype=jnp.int32)[None, :]
    flat_index = jnp.clip(sources * capacity + my_rank[:, None], 0, groups * capacity - 1)
    gathered = jnp.take(
        arrived.reshape(groups * capacity, width), flat_index.reshape(-1), axis=0
    ).reshape(tok_rows, D)
    segment_part = jnp.where(my_in[:, None], gathered.astype(jnp.float32), 0.0)
    slot_place = jnp.where(my_in, my_slot, PACK)
    token_at = (
        jnp.zeros((PACK, capacity), jnp.int32)
        .at[slot_place, my_rank]
        .set(jnp.arange(tok_rows, dtype=jnp.int32), mode="drop")
    )
    valid = jnp.zeros((PACK, capacity), jnp.bool_).at[slot_place, my_rank].set(True, mode="drop")
    grad_pick = jnp.take(whole_grad, token_at.reshape(-1), axis=0).reshape(
        PACK, capacity, quarters, width
    )
    grad_pick = jnp.where(valid[:, :, None, None], grad_pick, jnp.zeros((), jnp.bfloat16))
    grad_send = grad_pick.transpose(0, 2, 1, 3).reshape(groups, capacity, width)
    returned = lax.all_to_all(grad_send, "dp", split_axis=0, concat_axis=0, tiled=True)
    target = jnp.where(filled, row_of, lines)
    accum = (
        jnp.zeros((lines, width), jnp.float32)
        .at[target.reshape(-1)]
        .add(returned.reshape(-1, width).astype(jnp.float32), mode="drop")
    )
    embedded = lax.psum(segment_part.astype(jnp.bfloat16), "segment")
    return (embedded, accum.astype(jnp.bfloat16))


def solution(mesh):
    placed = (P("dp"), P("segment", "dp"), P("dp", "segment"))
    return jax.shard_map(
        body,
        mesh=mesh,
        in_specs=placed,
        out_specs=(P("dp", None), P("segment", "dp")),
        check_vma=False,
    )
```

profile of v0, /device:TPU:0, one launch (start us, length us, event | category | flops | bytes accessed | tf_op | source)
XLA Modules:
  0.0 159.1 jit_solution(7434590179938538914)
XLA Ops:
  7.2 22.6 %all-gather = s32[8,1,128]{2,1,0:T(1,128)S(1)} all-gather(s32[1,1,128]{2,1,0:T(1,128)} %bitcast.39), channel_id=1, replica_groups=mesh['segment'=4,'dp'=8] {'dp'}, dimensions={0}, use_global_device_ids=true | all-gather | bytes 4608 | tf_op jit(solution)/shard_map/all_gather | solution.py:18
  29.8 0.3 copy.12
  30.1 0.3 copy.13
  30.4 23.6 %compare_select_fusion = s32[8,128,1]{2,0,1:T(8,128)S(1)} fusion(pred[8,128,1]{2,0,1:T(8,128)(4,1)S(1)} %copy.13, s32[8,128,1]{2,0,1:T(8,128)S(1)} %copy.12), kind=kOutput, calls=%fused_computation.12 | output fusion | flops 135168 | bytes 9216 | tf_op jit(solution)/shard_map/jit(cumsum)/reduce_window_sum | solution.py:26
  54.0 0.2 copy.14
  54.2 0.8 multiply_reduce_fusion
  55.0 0.1 copy.19
  55.1 0.7 and_reduce_fusion
  55.8 0.1 copy.18
  56.0 4.3 %scatter_custom_fusion.4 = s32[128]{0:T(128)S(1)} fusion(s32[1024]{0:T(1024)S(1)} %bitcast.40, s32[1024]{0:T(1024)S(1)} %fusion.6, s32[]{:T(128)} %constant.70.clone.1), kind=kCustom, calls=%fused_computation.66 | custom fusion | bytes 516
  60.4 4.3 %scatter_custom_fusion.3 = pred[128]{0:T(512)(128)(4,1)S(1)} fusion(s32[1024]{0:T(1024)S(1)} %bitcast.41, pred[1024]{0:T(1024)(128)(4,1)S(1)} %broadcast.224, pred[]{:T(512)} %constant.71.clone.1), kind=kCustom, calls=%fused_computation.56 | custom fusion | bytes 129
  64.8 0.1 reshape.185
  64.9 6.6 %gather_fusion = bf16[128,3584]{1,0:T(8,128)(2,1)S(1)} fusion(bf16[1188,3584]{1,0:T(8,128)(2,1)} %param.6, s32[1024]{0:T(1024)S(1)} %pad_clamp_fusion.2), kind=kCustom, calls=%fused_computation.2 | custom fusion | bytes 1835520 | tf_op jit(solution)/shard_map/jit(_take)/gather | solution.py:35
  71.4 1.1 select_select_fusion
  72.6 3.6 %all-to-all-start = ((bf16[8,16,3584]{2,1,0:T(8,128)(2,1)}), bf16[8,16,3584]{2,1,0:T(8,128)(2,1)S(1)}, u32[]{:S(2)}, u32[]{:S(2)}) async-start(bf16[8,16,3584]{2,1,0:T(8,128)(2,1)} %select_select_fusion), calls=%async_computation | async-start | bytes 1835008 | tf_op jit(solution)/shard_map/all_to_all | solution.py:37
  76.2 0.1 fusion.4
  76.3 0.2 reduce_window_sum.23
  76.4 0.2 select_reduce_fusion
  76.7 6.4 %scatter_fusion.1 = s32[8,16]{1,0:T(8,128)S(1)} fusion(s32[8,16]{1,0:T(8,128)S(1)} %broadcast.169, s32[128]{0:T(128)S(1)} %fusion.18, s32[128]{0:T(128)S(1)} %iota.14), kind=kCustom, calls=%fused_computation.4 | custom fusion | bytes 2560 | tf_op jit(solution)/shard_map/scatter | solution.py:54
  83.0 0.1 reshape.180
  83.2 9.5 %all_gather.7 = bf16[128,3584]{1,0:T(8,128)(2,1)S(1)} all-gather(bf16[128,896]{1,0:T(8,128)(2,1)S(1)} %copy-done), channel_id=1, replica_groups=mesh['segment'=4,'dp'=8] {'segment'}, dimensions={1}, use_global_device_ids=true | all-gather | bytes 1146880 | tf_op jit(solution)/shard_map/all_gather | solution.py:23
  92.7 1.1 gather_fusion.2
  93.8 6.5 %scatter_fusion = pred[8,16]{1,0:T(8,128)(4,1)S(1)} fusion(pred[8,16]{1,0:T(8,128)(4,1)S(1)} %broadcast.166, s32[128]{0:T(128)S(1)} %fusion.18, pred[128]{0:T(512)(128)(4,1)S(1)} %broadcast.225), kind=kCustom, calls=%fused_computation.3 | custom fusion | bytes 1408 | tf_op jit(solution)/shard_map/scatter | solution.py:56
  100.3 0.2 broadcast_select_fusion
  100.5 1.1 broadcast_select_fusion.1
  101.5 5.9 %all-to-all-start.1 = ((bf16[8,16,3584]{2,1,0:T(8,128)(2,1)}), bf16[8,16,3584]{2,1,0:T(8,128)(2,1)S(1)}, u32[]{:S(2)}, u32[]{:S(2)}) async-start(bf16[8,16,3584]{2,1,0:T(8,128)(2,1)} %broadcast_select_fusion.1), calls=%async_computation.1 | async-start | bytes 1835008 | tf_op jit(solution)/shard_map/all_to_all | solution.py:62
  107.5 1.1 gather_fusion.1
  108.7 1.3 select_convert_fusion
  110.1 20.9 %all-to-all-done.1 = bf16[8,16,3584]{2,1,0:T(8,128)(2,1)S(1)} async-done(((bf16[8,16,3584]{2,1,0:T(8,128)(2,1)}), bf16[8,16,3584]{2,1,0:T(8,128)(2,1)S(1)}, u32[]{:S(2)}, u32[]{:S(2)}) %all-to-all-start.1) | async-done | bytes 917536 | tf_op jit(solution)/shard_map/all_to_all | solution.py:62
  130.9 10.0 %scatter_custom_fusion.2 = f32[1188,3584]{1,0:T(8,128)} fusion(s32[128]{0:T(128)S(1)} %fusion.16, f32[]{:T(128)} %constant.121.clone.1, bf16[128,3584]{1,0:T(8,128)(2,1)S(1)} %bitcast.35), kind=kCustom, calls=%fused_computation.8 | custom fusion | flops 917504 | bytes 17948676 | tf_op jit(solution)/shard_map/scatter-add | solution.py:67
  140.9 9.1 %convert_element_type.32 = bf16[1188,3584]{1,0:T(8,128)(2,1)} convert(f32[1188,3584]{1,0:T(8,128)} %scatter_custom_fusion.2) | non-fusion elementwise | flops 4257792 | bytes 25546752 | tf_op jit(solution)/shard_map/convert_element_type | solution.py:70
  150.1 2.2 %copy.23 = bf16[128,3584]{1,0:T(8,128)(2,1)} copy(bf16[128,3584]{1,0:T(8,128)(2,1)} %all-reduce.2.cloned.1.call-done) | data formatting | bytes 1835008
  (34 shorter events, 0.5 us)
Async XLA Ops:
  7.2 69.0 %copy-start.1 = (s32[128]{0:T(128)S(1)}, s32[128]{0:T(128)}, u32[]{:S(2)}) copy-start(s32[128]{0:T(128)} %param.5) | copy-start | bytes 1540
  7.2 76.0 %copy-start = (bf16[128,896]{1,0:T(8,128)(2,1)S(1)}, bf16[128,896]{1,0:T(8,128)(2,1)}, u32[]{:S(2)}) copy-start(bf16[128,896]{1,0:T(8,128)(2,1)} %param.7) | copy-start | bytes 688132
  72.6 29.0 %all-to-all-start = ((bf16[8,16,3584]{2,1,0:T(8,128)(2,1)}), bf16[8,16,3584]{2,1,0:T(8,128)(2,1)S(1)}, u32[]{:S(2)}, u32[]{:S(2)}) async-start(bf16[8,16,3584]{2,1,0:T(8,128)(2,1)} %select_select_fusion), calls=%async_computation | async-start | bytes 1835008 | tf_op jit(solution)/shard_map/all_to_all | solution.py:37
  101.5 29.4 %all-to-all-start.1 = ((bf16[8,16,3584]{2,1,0:T(8,128)(2,1)}), bf16[8,16,3584]{2,1,0:T(8,128)(2,1)S(1)}, u32[]{:S(2)}, u32[]{:S(2)}) async-start(bf16[8,16,3584]{2,1,0:T(8,128)(2,1)} %broadcast_select_fusion.1), calls=%async_computation.1 | async-start | bytes 1835008 | tf_op jit(solution)/shard_map/all_to_all | solution.py:62
  107.5 42.6 %all-reduce.2.cloned.1.call-start = ((), (), s32[]{:S(2)}) async-start(), calls=%async_computation.2 | async-start | bytes 1835008 | tf_op jit(solution)/shard_map/psum | solution.py:69
Sparse Core Ops, SparseCore 0:
  111.2 36.2 all-reduce.1
where the time goes:
time: 159 us
  other arithmetic  48.5 us (31%)
  local copies, waits for them, and re-layouts  33.8 us (21%)
  blocking collectives  32.1 us (20%)
  waiting for transfers between devices  20.9 us (13%)
  between operations  14.3 us (9%)
  starting transfers between devices  9.52 us (6%)
    another operation x1, other arithmetic, body(): rank = jnp.cumsum(owned_grid.astype(jnp.int32), axis=1) - 1  23.6 us
    all_gather x1, blocking collectives, body(): every_id = lax.all_gather(token_ids, 'dp', axis=0, tiled=True)  22.6 us
    all_to_all x1, waiting for transfers between devices, body(): lax.all_to_all(grad_send, 'dp', split_axis=0, concat_axis=0, tiled=True)  20.9 us
    unnamed x11, local copies, waits for them, and re-layouts  11.1 us
    scatter-add x1, other arithmetic, body(): accum = jnp.zeros((lines, width), jnp.float32).at[target.reshape(-1)].add...  10 us
    all_gather x1, blocking collectives, body(): whole_grad = lax.all_gather(out_grad, 'segment', axis=1, tiled=True)  9.52 us
    convert_element_type x1, other arithmetic, body(): return (embedded, accum.astype(jnp.bfloat16))  9.14 us
    gather x1, local copies, waits for them, and re-layouts, body(): jnp.take(table, row_of.reshape(-1), axis=0).reshape(groups, capacity, width)  6.55 us
  transfers between devices with their start and end apart: 3, of which 1 were waited for; matrix products, arithmetic and copies ran while one was open for 24% of the time, Pallas kernels for 0%

commit v1 on v0

--- a/solution.py
+++ b/solution.py
@@ -5,6 +5,33 @@
 
 D = 3584
 PACK = 8
+
+
+def tell_patch(local_array, out_dim):
+    state_next = lax.axis_index("dp")
+    z = lax.axis_size("dp")
+    last, taken_in, answer = (z, state_next, local_array.shape[out_dim])
+    stack_in = [
+        tick * last if num == out_dim else tick for num, tick in enumerate(local_array.shape)
+    ]
+    val = jnp.zeros(stack_in, local_array.dtype)
+    u1 = u_next = local_array
+    rr = 1
+    k_now = lax.dynamic_update_slice_in_dim(val, local_array, taken_in * answer, axis=out_dim)
+    while rr < last // 2 + 1:
+        u1 = lax.ppermute(u1, "dp", perm=[(num, (num + 1) % last) for num in range(last)])
+        k_now = lax.dynamic_update_slice_in_dim(
+            k_now, u1, (taken_in - rr) % last * answer, axis=out_dim
+        )
+        if 2 * rr < last:
+            u_next = lax.ppermute(
+                u_next, "dp", perm=[(num, (num - 1) % last) for num in range(last)]
+            )
+            k_now = lax.dynamic_update_slice_in_dim(
+                k_now, u_next, (taken_in + rr) % last * answer, axis=out_dim
+            )
+        rr += 1
+    return k_now
 
 
 def body(token_ids, table, out_grad):
@@ -15,7 +42,7 @@
     quarters = D // width
     slot = lax.axis_index("dp") // quarters
     first = lax.axis_index("segment") * lines * PACK
-    every_id = lax.all_gather(token_ids, "dp", axis=0, tiled=True)
+    every_id = tell_patch(token_ids, 0)
     local = every_id - first
     in_section = (local >= 0) & (local < lines * PACK)
     owned = in_section & (local % PACK == slot)

time: 159 us -> 177 us (1.11)
  blocking collectives: 32.1 us -> 9.68 us
  waiting for transfers between devices: 20.9 us -> 42.3 us
  starting transfers between devices: 9.52 us -> 25.2 us
  local copies, waits for them, and re-layouts: 33.8 us -> 36.3 us
    all_gather x1 -> x0, blocking collectives: 22.6 us -> none  [body(): every_id = lax.all_gather(token_ids, 'dp', axis=0, tiled=True)]
    all_to_all x1, waiting for transfers between devices: 0.01 us -> 20.5 us  [body(): lax.all_to_all(fetched, 'dp', split_axis=0, concat_axis=0, tiled=True)]
    ppermute x0 -> x7, starting transfers between devices: none -> 15.6 us  [the longest x3 12.6 us: tell_patch(): lax.ppermute(u_next, 'dp', perm=[(num, (num - 1) % last) for num in range...]
    all_to_all x1, starting transfers between devices: 3.55 us -> 6 us  [body(): lax.all_to_all(fetched, 'dp', split_axis=0, concat_axis=0, tiled=True)]
    all_to_all x1, starting transfers between devices: 5.93 us -> 3.55 us  [body(): lax.all_to_all(grad_send, 'dp', split_axis=0, concat_axis=0, tiled=True)]
    dynamic_update_slice x0 -> x8, local copies, waits for them, and re-layouts: none -> 2.31 us  [the longest x4 0.86 us: tell_patch(): lax.dynamic_update_slice_in_dim(k_now, u1, (taken_in - rr) % last * answe...]
    unnamed x11 -> x13, local copies, waits for them, and re-layouts: 11.1 us -> 11.3 us
  transfers between devices with their start and end apart: 3 -> 10, of which waited for: 1 -> 3; matrix products, arithmetic and copies ran while one was open for 24% -> 24% of each run, Pallas kernels for 0% -> 0%
where the time goes in v1:
time: 177 us
  other arithmetic  49 us (28%)
  waiting for transfers between devices  42.3 us (24%)
  local copies, waits for them, and re-layouts  36.3 us (21%)
  starting transfers between devices  25.2 us (14%)
  between operations  14.3 us (8%)
  blocking collectives  9.68 us (5%)
    another operation x1, other arithmetic, body(): rank = jnp.cumsum(owned_grid.astype(jnp.int32), axis=1) - 1  23.3 us
    all_to_all x1, waiting for transfers between devices, body(): lax.all_to_all(fetched, 'dp', split_axis=0, concat_axis=0, tiled=True)  20.5 us
    all_to_all x1, waiting for transfers between devices, body(): lax.all_to_all(grad_send, 'dp', split_axis=0, concat_axis=0, tiled=True)  20.3 us
    ppermute x3, starting transfers between devices, tell_patch(): lax.ppermute(u_next, 'dp', perm=[(num, (num - 1) % last) for num in range...  12.6 us
    unnamed x13, local copies, waits for them, and re-layouts  11.3 us
    scatter-add x1, other arithmetic, body(): accum = jnp.zeros((lines, width), jnp.float32).at[target.reshape(-1)].add...  10 us
    all_gather x1, blocking collectives, body(): whole_grad = lax.all_gather(out_grad, 'segment', axis=1, tiled=True)  9.68 us
    convert_element_type x1, other arithmetic, body(): return (embedded, accum.astype(jnp.bfloat16))  9.14 us
  transfers between devices with their start and end apart: 10, of which 3 were waited for; matrix products, arithmetic and copies ran while one was open for 24% of the time, Pallas kernels for 0%

profile of v1, /device:TPU:0, one launch (start us, length us, event | category | flops | bytes accessed | tf_op | source)
XLA Modules:
  0.0 176.8 jit_solution(16571594506045374793)
XLA Ops:
  7.2 3.0 %collective-permute-start = (s32[128]{0:T(128)}, s32[128]{0:T(128)S(1)}, u32[]{:S(2)}, u32[]{:S(2)}) collective-permute-start(s32[128]{0:T(128)} %param.5), channel_id=1, source_target_pairs={{0,1},{1,2},{2,3},{3,4},{4,5},{5,6},{6,7},{7,0},{8,9},{9,10},{10,1... | collective-permute-start | bytes 1544 | tf_op jit(solution)/shard_map/ppermute | solution.py:22
  10.2 3.1 %collective-permute-start.1 = (s32[128]{0:T(128)}, s32[128]{0:T(128)S(1)}, u32[]{:S(2)}, u32[]{:S(2)}) collective-permute-start(s32[128]{0:T(128)} %param.5), channel_id=1, source_target_pairs={{0,7},{1,0},{2,1},{3,2},{4,3},{5,4},{6,5},{7,6},{8,15},{9,8},{10,9... | collective-permute-start | bytes 1544 | tf_op jit(solution)/shard_map/ppermute | solution.py:27
  13.3 0.7 compare_and_fusion.3
  14.0 0.7 and_select_fusion
  15.1 0.7 fusion.18
  15.8 6.4 %scatter_fusion.1 = s32[8,16]{1,0:T(8,128)S(1)} fusion(s32[8,16]{1,0:T(8,128)S(1)} %broadcast.180, s32[128]{0:T(128)S(1)} %fusion.18, s32[128]{0:T(128)S(1)} %iota.14), kind=kCustom, calls=%fused_computation.4 | custom fusion | bytes 2560 | tf_op jit(solution)/shard_map/scatter | solution.py:81
  22.3 9.7 %all_gather.3 = bf16[128,3584]{1,0:T(8,128)(2,1)S(1)} all-gather(bf16[128,896]{1,0:T(8,128)(2,1)} %param.7), channel_id=1, replica_groups=mesh['segment'=4,'dp'=8] {'segment'}, dimensions={1}, use_global_device_ids=true | all-gather | bytes 1146880 | tf_op jit(solution)/shard_map/all_gather | solution.py:50
  32.0 4.7 %collective-permute-start.3 = (s32[128]{0:T(128)S(1)}, s32[128]{0:T(128)S(1)}, u32[]{:S(2)}, u32[]{:S(2)}) collective-permute-start(s32[128]{0:T(128)S(1)} %collective-permute-done.1), channel_id=1, source_target_pairs={{0,7},{1,0},{2,1},{3,2},{4,3},{5,4},{6,5},{7,6},{8,15},{9,8},{10,9... | collective-permute-start | bytes 1544 | tf_op jit(solution)/shard_map/ppermute | solution.py:27
  36.7 1.5 collective-permute-done.2
  38.3 0.8 dynamic_update_slice.24
  39.1 1.1 gather_fusion.2
  40.2 4.8 %collective-permute-start.5 = (s32[128]{0:T(128)S(1)}, s32[128]{0:T(128)S(1)}, u32[]{:S(2)}, u32[]{:S(2)}) collective-permute-start(s32[128]{0:T(128)S(1)} %collective-permute-done.3), channel_id=1, source_target_pairs={{0,7},{1,0},{2,1},{3,2},{4,3},{5,4},{6,5},{7,6},{8,15},{9,8},{10,9... | collective-permute-start | bytes 1544 | tf_op jit(solution)/shard_map/ppermute | solution.py:27
  45.0 6.5 %scatter_fusion = pred[8,16]{1,0:T(8,128)(4,1)S(1)} fusion(pred[8,16]{1,0:T(8,128)(4,1)S(1)} %broadcast.176, s32[128]{0:T(128)S(1)} %fusion.18, pred[128]{0:T(512)(128)(4,1)S(1)} %broadcast.236), kind=kCustom, calls=%fused_computation.3 | custom fusion | bytes 1408 | tf_op jit(solution)/shard_map/scatter | solution.py:83
  51.5 0.2 dynamic_update_slice.25
  52.6 0.2 dynamic_update_slice.30
  53.0 0.3 copy.12
  53.3 23.3 %fusion.23 = s32[8,128,1]{2,0,1:T(8,128)S(1)} fusion(s32[8,128,1]{2,0,1:T(8,128)S(1)} %copy.12), kind=kOutput, calls=%fused_computation.69 | output fusion | flops 130048 | bytes 8192 | tf_op jit(solution)/shard_map/jit(cumsum)/reduce_window_sum | solution.py:53
  76.6 0.3 copy.13
  77.7 4.3 %scatter_custom_fusion.4 = s32[128]{0:T(128)S(1)} fusion(s32[1024]{0:T(1024)S(1)} %bitcast.32, s32[1024]{0:T(1024)S(1)} %fusion.6, s32[]{:T(128)} %constant.145.clone.1), kind=kCustom, calls=%fused_computation.66 | custom fusion | bytes 516
  82.1 4.5 %scatter_custom_fusion.3 = pred[128]{0:T(512)(128)(4,1)S(1)} fusion(s32[1024]{0:T(1024)S(1)} %bitcast.33, pred[1024]{0:T(1024)(128)(4,1)S(1)} %broadcast.235, pred[]{:T(512)} %constant.146.clone.1), kind=kCustom, calls=%fused_computation.56 | custom fusion | bytes 129
  86.8 6.6 %gather_fusion = bf16[128,3584]{1,0:T(8,128)(2,1)S(1)} fusion(bf16[1188,3584]{1,0:T(8,128)(2,1)} %param.6, s32[1024]{0:T(1024)S(1)} %pad_clamp_fusion.2), kind=kCustom, calls=%fused_computation.2 | custom fusion | bytes 1835520 | tf_op jit(solution)/shard_map/jit(_take)/gather | solution.py:62
  93.4 1.1 select_select_fusion
  94.5 6.0 %all-to-all-start = ((bf16[8,16,3584]{2,1,0:T(8,128)(2,1)}), bf16[8,16,3584]{2,1,0:T(8,128)(2,1)S(1)}, u32[]{:S(2)}, u32[]{:S(2)}) async-start(bf16[8,16,3584]{2,1,0:T(8,128)(2,1)} %select_select_fusion), calls=%async_computation | async-start | bytes 1835008 | tf_op jit(solution)/shard_map/all_to_all | solution.py:64
  100.6 1.1 broadcast_select_fusion.1
  101.7 20.5 %all-to-all-done = bf16[8,16,3584]{2,1,0:T(8,128)(2,1)S(1)} async-done(((bf16[8,16,3584]{2,1,0:T(8,128)(2,1)}), bf16[8,16,3584]{2,1,0:T(8,128)(2,1)S(1)}, u32[]{:S(2)}, u32[]{:S(2)}) %all-to-all-start) | async-done | bytes 917536 | tf_op jit(solution)/shard_map/all_to_all | solution.py:64
  122.2 3.6 %all-to-all-start.1 = ((bf16[8,16,3584]{2,1,0:T(8,128)(2,1)}), bf16[8,16,3584]{2,1,0:T(8,128)(2,1)S(1)}, u32[]{:S(2)}, u32[]{:S(2)}) async-start(bf16[8,16,3584]{2,1,0:T(8,128)(2,1)} %broadcast_select_fusion.1), calls=%async_computation.1 | async-start | bytes 1835008 | tf_op jit(solution)/shard_map/all_to_all | solution.py:89
  125.8 1.1 gather_fusion.1
  127.0 1.3 select_convert_fusion
  128.4 20.3 %all-to-all-done.1 = bf16[8,16,3584]{2,1,0:T(8,128)(2,1)S(1)} async-done(((bf16[8,16,3584]{2,1,0:T(8,128)(2,1)}), bf16[8,16,3584]{2,1,0:T(8,128)(2,1)S(1)}, u32[]{:S(2)}, u32[]{:S(2)}) %all-to-all-start.1) | async-done | bytes 917536 | tf_op jit(solution)/shard_map/all_to_all | solution.py:89
  148.6 10.0 %scatter_custom_fusion.2 = f32[1188,3584]{1,0:T(8,128)} fusion(s32[128]{0:T(128)S(1)} %fusion.16, f32[]{:T(128)} %constant.166.clone.1, bf16[128,3584]{1,0:T(8,128)(2,1)S(1)} %bitcast.31), kind=kCustom, calls=%fused_computation.8 | custom fusion | flops 917504 | bytes 17948676 | tf_op jit(solution)/shard_map/scatter-add | solution.py:94
  158.7 9.1 %convert_element_type.32 = bf16[1188,3584]{1,0:T(8,128)(2,1)} convert(f32[1188,3584]{1,0:T(8,128)} %scatter_custom_fusion.2) | non-fusion elementwise | flops 4257792 | bytes 25546752 | tf_op jit(solution)/shard_map/convert_element_type | solution.py:97
  167.8 2.2 %copy.31 = bf16[128,3584]{1,0:T(8,128)(2,1)} copy(bf16[128,3584]{1,0:T(8,128)(2,1)} %all-reduce.2.cloned.1.call-done) | data formatting | bytes 1835008
  (58 shorter events, 2.9 us)
Async XLA Ops:
  7.2 70.1 %copy-start.2 = (s32[2]{0:T(128)S(1)}, s32[2]{0:T(128)}, u32[]{:S(2)}) copy-start(s32[2]{0:T(128)} %constant.167) | copy-start | bytes 28
  7.2 70.3 %copy-start.1 = (s32[2]{0:T(128)S(1)}, s32[2]{0:T(128)}, u32[]{:S(2)}) copy-start(s32[2]{0:T(128)} %constant.170) | copy-start | bytes 28
  7.2 24.8 %collective-permute-start = (s32[128]{0:T(128)}, s32[128]{0:T(128)S(1)}, u32[]{:S(2)}, u32[]{:S(2)}) collective-permute-start(s32[128]{0:T(128)} %param.5), channel_id=1, source_target_pairs={{0,1},{1,2},{2,3},{3,4},{4,5},{5,6},{6,7},{7,0},{8,9},{9,10},{10,1... | collective-permute-start | bytes 1544 | tf_op jit(solution)/shard_map/ppermute | solution.py:22
  10.2 21.8 %collective-permute-start.1 = (s32[128]{0:T(128)}, s32[128]{0:T(128)S(1)}, u32[]{:S(2)}, u32[]{:S(2)}) collective-permute-start(s32[128]{0:T(128)} %param.5), channel_id=1, source_target_pairs={{0,7},{1,0},{2,1},{3,2},{4,3},{5,4},{6,5},{7,6},{8,15},{9,8},{10,9... | collective-permute-start | bytes 1544 | tf_op jit(solution)/shard_map/ppermute | solution.py:27
  32.0 6.3 %collective-permute-start.2 = (s32[128]{0:T(128)S(1)}, s32[128]{0:T(128)S(1)}, u32[]{:S(2)}, u32[]{:S(2)}) collective-permute-start(s32[128]{0:T(128)S(1)} %collective-permute-done), channel_id=1, source_target_pairs={{0,1},{1,2},{2,3},{3,4},{4,5},{5,6},{6,7},{7,0},{8,9},{9,10},{10,1... | collective-permute-start | bytes 1544 | tf_op jit(solution)/shard_map/ppermute | solution.py:22
  32.0 8.2 %collective-permute-start.3 = (s32[128]{0:T(128)S(1)}, s32[128]{0:T(128)S(1)}, u32[]{:S(2)}, u32[]{:S(2)}) collective-permute-start(s32[128]{0:T(128)S(1)} %collective-permute-done.1), channel_id=1, source_target_pairs={{0,7},{1,0},{2,1},{3,2},{4,3},{5,4},{6,5},{7,6},{8,15},{9,8},{10,9... | collective-permute-start | bytes 1544 | tf_op jit(solution)/shard_map/ppermute | solution.py:27
  38.3 6.7 %collective-permute-start.4 = (s32[128]{0:T(128)S(1)}, s32[128]{0:T(128)S(1)}, u32[]{:S(2)}, u32[]{:S(2)}) collective-permute-start(s32[128]{0:T(128)S(1)} %collective-permute-done.2), channel_id=1, source_target_pairs={{0,1},{1,2},{2,3},{3,4},{4,5},{5,6},{6,7},{7,0},{8,9},{9,10},{10,1... | collective-permute-start | bytes 1544 | tf_op jit(solution)/shard_map/ppermute | solution.py:22
  40.2 12.3 %collective-permute-start.5 = (s32[128]{0:T(128)S(1)}, s32[128]{0:T(128)S(1)}, u32[]{:S(2)}, u32[]{:S(2)}) collective-permute-start(s32[128]{0:T(128)S(1)} %collective-permute-done.3), channel_id=1, source_target_pairs={{0,7},{1,0},{2,1},{3,2},{4,3},{5,4},{6,5},{7,6},{8,15},{9,8},{10,9... | collective-permute-start | bytes 1544 | tf_op jit(solution)/shard_map/ppermute | solution.py:27
  45.0 7.8 %collective-permute-start.6 = (s32[128]{0:T(128)S(1)}, s32[128]{0:T(128)S(1)}, u32[]{:S(2)}, u32[]{:S(2)}) collective-permute-start(s32[128]{0:T(128)S(1)} %collective-permute-done.4), channel_id=1, source_target_pairs={{0,1},{1,2},{2,3},{3,4},{4,5},{5,6},{6,7},{7,0},{8,9},{9,10},{10,1... | collective-permute-start | bytes 1544 | tf_op jit(solution)/shard_map/ppermute | solution.py:22
  86.8 39.0 %copy-start = (s32[128]{0:T(128)S(1)}, s32[128]{0:T(128)}, u32[]{:S(2)}) copy-start(s32[128]{0:T(128)} %param.5) | copy-start | bytes 1540
  94.5 27.7 %all-to-all-start = ((bf16[8,16,3584]{2,1,0:T(8,128)(2,1)}), bf16[8,16,3584]{2,1,0:T(8,128)(2,1)S(1)}, u32[]{:S(2)}, u32[]{:S(2)}) async-start(bf16[8,16,3584]{2,1,0:T(8,128)(2,1)} %select_select_fusion), calls=%async_computation | async-start | bytes 1835008 | tf_op jit(solution)/shard_map/all_to_all | solution.py:64
  122.2 26.4 %all-to-all-start.1 = ((bf16[8,16,3584]{2,1,0:T(8,128)(2,1)}), bf16[8,16,3584]{2,1,0:T(8,128)(2,1)S(1)}, u32[]{:S(2)}, u32[]{:S(2)}) async-start(bf16[8,16,3584]{2,1,0:T(8,128)(2,1)} %broadcast_select_fusion.1), calls=%async_computation.1 | async-start | bytes 1835008 | tf_op jit(solution)/shard_map/all_to_all | solution.py:89
  125.7 42.0 %all-reduce.2.cloned.1.call-start = ((), (), s32[]{:S(2)}) async-start(), calls=%async_computation.2 | async-start | bytes 1835008 | tf_op jit(solution)/shard_map/psum | solution.py:96
Sparse Core Ops, SparseCore 0:
  129.5 36.2 all-reduce.1
